TPU v7x, 128 devices: a whole 4x4x4 slice. The times are simulated.
128 devices in a mesh: shard: 16 (over z_hi, x, core), tp: 8 (over z_lo, y).
Axes of the slice: x: 4, y: 4, z: 4 (z_hi: 2, z_lo: 2; z = z_hi * 2 + z_lo), core: 2. Of those that a mesh axis runs over, the one named last changes fastest.
Arguments:
- train_query: bfloat16 [5120, 8192], P('shard', 'tp'), may hold values from -0.078125 to 0.078125
- low_query: bfloat16 [5120, 32], P('shard'), may hold values from -0.078125 to 0.078125
- high_query: bfloat16 [32, 8192], P(None, 'tp'), may hold values from -1 to 1
- train_key: bfloat16 [5120, 1024], P('shard', 'tp'), may hold values from -0.078125 to 0.078125
- low_key: bfloat16 [5120, 32], P('shard'), may hold values from -0.078125 to 0.078125
- high_key: bfloat16 [32, 1024], P(None, 'tp'), may hold values from -1 to 1
- train_value: bfloat16 [5120, 1024], P('shard', 'tp'), may hold values from -0.078125 to 0.078125
- low_value: bfloat16 [5120, 32], P('shard'), may hold values from -0.078125 to 0.078125
- high_value: bfloat16 [32, 1024], P(None, 'tp'), may hold values from -1 to 1
- train_mixed: bfloat16 [8192, 5120], P('tp', 'shard'), may hold values from -0.0625 to 0.0625
- low_mixed: bfloat16 [8192, 32], P('tp'), may hold values from -0.0625 to 0.0625
- high_mixed: bfloat16 [32, 5120], P(None, 'shard'), may hold values from -1 to 1
- norm_train: float32 [5120], P(('shard', 'tp')), may hold values from 0.25 to 1.75
- norm_step: float32 [5120], P(('shard', 'tp')), may hold values from -0.3 to 0.3
Outputs:
- final_query: bfloat16 [5120, 8192], P(None, 'tp')
- final_key: bfloat16 [5120, 1024], P(None, 'tp')
- final_value: bfloat16 [5120, 1024], P(None, 'tp')
- final_mixed: bfloat16 [8192, 5120], P('tp')
- serve_norm: bfloat16 [5120], replicated
All inputs are finite; a program needn't handle non-finite values.
Results may differ from a plain program's by a relative error of at most 0.001.
Values may be sent and summed in bfloat16 or wider, within the bound.
A program may use at most 128 MiB of HBM per device.

v0:
```python
import jax
import jax.numpy as jnp
from jax import lax
from jax.sharding import PartitionSpec as P

mix_rate = 0.5


def rows_first(arrays, axis, dims):
    turned = [jnp.moveaxis(a, dim, 0) for a, dim in zip(arrays, dims)]
    widths = [t[0].size for t in turned]
    both = jnp.concatenate([t.reshape(-1, w) for t, w in zip(turned, widths)], axis=1)
    out = lax.all_gather(both, axis, axis=0, tiled=True)
    parts = jnp.split(out, [sum(widths[:k]) for k in range(1, len(widths))], axis=1)
    return tuple(
        (
            jnp.moveaxis(b.reshape(-1, *t.shape[1:]), 0, dim)
            for b, t, dim in zip(parts, turned, dims)
        )
    )


def body(
    train_query,
    low_query,
    high_query,
    train_key,
    low_key,
    high_key,
    train_value,
    low_value,
    high_value,
    train_mixed,
    low_mixed,
    high_mixed,
    norm_train,
    norm_step,
):
    result_query = train_query.astype(jnp.float32) + mix_rate * jnp.dot(
        low_query, high_query, preferred_element_type=jnp.float32
    )
    result_key = train_key.astype(jnp.float32) + mix_rate * jnp.dot(
        low_key, high_key, preferred_element_type=jnp.float32
    )
    result_value = train_value.astype(jnp.float32) + mix_rate * jnp.dot(
        low_value, high_value, preferred_element_type=jnp.float32
    )
    result_mixed = train_mixed.astype(jnp.float32) + mix_rate * jnp.dot(
        low_mixed, high_mixed, preferred_element_type=jnp.float32
    )
    narrow_query, narrow_key, narrow_value, narrow_mixed = (
        result_query.astype(jnp.bfloat16),
        result_key.astype(jnp.bfloat16),
        result_value.astype(jnp.bfloat16),
        result_mixed.astype(jnp.bfloat16),
    )
    final_query, final_key, final_value, final_mixed = rows_first(
        (narrow_query, narrow_key, narrow_value, narrow_mixed), "shard", (0, 0, 0, 1)
    )
    serve_norm = lax.all_gather(
        (norm_train + norm_step).astype(jnp.bfloat16), ("shard", "tp"), axis=0, tiled=True
    )
    return (final_query, final_key, final_value, final_mixed, serve_norm)


def solution(mesh):
    return jax.shard_map(
        body,
        mesh=mesh,
        in_specs=(
            P("shard", "tp"),
            P("shard", None),
            P(None, "tp"),
            P("shard", "tp"),
            P("shard", None),
            P(None, "tp"),
            P("shard", "tp"),
            P("shard", None),
            P(None, "tp"),
            P("tp", "shard"),
            P("tp", None),
            P(None, "shard"),
            P(("shard", "tp")),
            P(("shard", "tp")),
        ),
        out_specs=(P(None, "tp"), P(None, "tp"), P(None, "tp"), P("tp", None), P()),
        check_vma=False,
    )
```

profile of v0, /device:TPU:1, one launch (start us, length us, event | category | flops | bytes accessed | tf_op | source)
XLA Modules:
  0.0 198.9 jit_solution(14225677418639521225)
XLA Ops:
  7.2 0.0 copy-start
  7.2 0.0 copy-start.4
  7.2 0.0 copy-start.6
  7.2 0.0 copy-start.2
  7.2 0.0 copy-start.5
  7.2 0.0 copy-start.3
  7.2 0.0 copy-start.1
  7.2 0.0 all-gather.2.cloned.1.call-start
  7.3 0.7 copy-done
  8.0 1.5 fusion.4
  9.5 1.1 fusion.8
  10.6 0.0 copy-done.4
  10.6 0.0 copy-done.6
  10.6 0.0 copy-done.2
  10.7 0.2 fusion.7
  10.9 0.0 copy-done.5
  10.9 0.0 copy-done.3
  10.9 0.0 copy-done.1
  10.9 0.4 fusion.2
  11.3 1.2 pad_maximum_fusion
  12.5 0.0 copy-start.7
  12.5 0.0 copy-start.8
  12.5 0.0 all-gather.2.cloned.1.call-update
  12.5 0.6 copy-done.7
  13.1 0.0 copy-done.8
  13.2 0.2 dynamic-update-slice
  13.4 139.6 %all-reduce = bf16[5120]{0:T(1024)(128)(2,1)} all-reduce(bf16[5120]{0:T(1024)(128)(2,1)S(1)} %dynamic-update-slice), channel_id=1, replica_groups=mesh['shard'=16,'tp'=8] {'shard','tp'}, use_global_device_ids=true, to_apply=%add | all-reduce | flops 5120 | bytes 20480
  153.0 5.9 %all-gather.2.cloned.1.call-done = bf16[5120,2304]{1,0:T(8,128)(2,1)} async-done(((bf16[320,2304]{1,0:T(8,128)(2,1)}), bf16[5120,2304]{1,0:T(8,128)(2,1)}) %all-gather.2.cloned.1.call-update) | async-done | bytes 23592976 | tf_op jit(solution)/shard_map/all_gather | solution.py:13
  158.8 16.2 %slice_bitcast_fusion = (bf16[1024,5120]{0,1:T(8,128)(2,1)}, bf16[5120,1024]{1,0:T(8,128)(2,1)}) fusion(bf16[5120,2304]{1,0:T(8,128)(2,1)} %all-gather.2.cloned.1.call-done), kind=kLoop, calls=%fused_computation | loop fusion | bytes 41943040 | tf_op jit(solution)/shard_map/transpose | solution.py:17
  175.0 13.7 %copy.19 = bf16[1024,5120]{1,0:T(8,128)(2,1)} copy(bf16[1024,5120]{0,1:T(8,128)(2,1)} %get-tuple-element.10) | data formatting | bytes 20971520
  188.7 3.4 %fusion.9 = (bf16[5120,128]{1,0:T(8,128)(2,1)}, bf16[5120,128]{1,0:T(8,128)(2,1)}) fusion(bf16[5120,2304]{1,0:T(8,128)(2,1)} %all-gather.2.cloned.1.call-done), kind=kLoop, calls=%fused_computation.16 | loop fusion | bytes 5242880 | tf_op jit(solution)/shard_map/split | solution.py:14
  (2 shorter events, 0.0 us)
Async XLA Ops:
  7.2 0.8 copy-start
  7.2 3.4 %copy-start.4 = (bf16[320,32]{0,1:T(8,128)(2,1)S(1)}, bf16[320,32]{0,1:T(8,128)(2,1)}, u32[]{:S(2)}) copy-start(bf16[320,32]{0,1:T(8,128)(2,1)} %param.18) | copy-start | bytes 61444
  7.2 3.4 %copy-start.6 = (bf16[32,128]{1,0:T(8,128)(2,1)S(1)}, bf16[32,128]{1,0:T(8,128)(2,1)}, u32[]{:S(2)}) copy-start(bf16[32,128]{1,0:T(8,128)(2,1)} %param.19) | copy-start | bytes 24580
  7.2 3.4 %copy-start.2 = (bf16[320,128]{1,0:T(8,128)(2,1)S(1)}, bf16[320,128]{1,0:T(8,128)(2,1)}, u32[]{:S(2)}) copy-start(bf16[320,128]{1,0:T(8,128)(2,1)} %param.17) | copy-start | bytes 245764
  7.2 3.7 %copy-start.5 = (bf16[320,32]{0,1:T(8,128)(2,1)S(1)}, bf16[320,32]{0,1:T(8,128)(2,1)}, u32[]{:S(2)}) copy-start(bf16[320,32]{0,1:T(8,128)(2,1)} %param.15) | copy-start | bytes 61444
  7.2 3.7 %copy-start.3 = (bf16[32,1024]{1,0:T(8,128)(2,1)S(1)}, bf16[32,1024]{1,0:T(8,128)(2,1)}, u32[]{:S(2)}) copy-start(bf16[32,1024]{1,0:T(8,128)(2,1)} %param.16) | copy-start | bytes 196612
  7.2 3.7 %copy-start.1 = (bf16[320,1024]{1,0:T(8,128)(2,1)S(1)}, bf16[320,1024]{1,0:T(8,128)(2,1)}, u32[]{:S(2)}) copy-start(bf16[320,1024]{1,0:T(8,128)(2,1)} %param.14) | copy-start | bytes 1966084
  7.2 151.6 %all-gather.2.cloned.1.call-start = ((), (), s32[]{:S(2)}) async-start(), calls=%async_computation | async-start | bytes 25067520 | tf_op jit(solution)/shard_map/all_gather | solution.py:13
  12.5 0.7 copy-start.7
  12.5 0.7 copy-start.8
Sparse Core Ops, SparseCore 0:
  12.6 146.1 all-gather.1
where the time goes:
time: 200 us; the launch traced here: 199 us
  blocking collectives  140 us (70%)
  local copies, waits for them, and re-layouts  34.9 us (17%)
  between operations  14.2 us (7%)
  waiting for transfers between devices  5.87 us (3%)
  matrix products  3.16 us (2%)
    unnamed x1, blocking collectives  140 us
    transpose x1, local copies, waits for them, and re-layouts, rows_first(): jnp.moveaxis(b.reshape(-1, *t.shape[1:]), 0, dim)  16.2 us
    unnamed x21, local copies, waits for them, and re-layouts  15.3 us
    all_gather x1, waiting for transfers between devices, rows_first(): out = lax.all_gather(both, axis, axis=0, tiled=True)  5.85 us
  transfers between devices with their start and end apart: 1, of which 1 were waited for; matrix products, arithmetic and copies ran while one was open for 0% of the time, Pallas kernels for 0%

commit v1 on v0

--- a/solution.py
+++ b/solution.py
@@ -10,7 +10,9 @@
     turned = [jnp.moveaxis(a, dim, 0) for a, dim in zip(arrays, dims)]
     widths = [t[0].size for t in turned]
     both = jnp.concatenate([t.reshape(-1, w) for t, w in zip(turned, widths)], axis=1)
-    out = lax.all_gather(both, axis, axis=0, tiled=True)
+    out = jnp.concatenate(
+        lax.all_to_all(jnp.stack([both] * lax.axis_size(axis)), axis, 0, 0), axis=0
+    )
     parts = jnp.split(out, [sum(widths[:k]) for k in range(1, len(widths))], axis=1)
     return tuple(
         (

time: 200 us -> 427 us (2.13)
  blocking collectives: 140 us -> 371 us
  between operations: 14.2 us -> 0.8 us
  starting transfers between devices: 0.04 us -> 9.25 us
  local copies, waits for them, and re-layouts: 34.9 us -> 42.5 us
  waiting for transfers between devices: 5.87 us -> 0.01 us
    unnamed x1, blocking collectives: 140 us -> 371 us
    all_to_all x0 -> x1, starting transfers between devices: none -> 9.25 us  [rows_first(): lax.all_to_all(jnp.stack([both] * lax.axis_size(axis)), axis, 0, 0)]
    another operation x0 -> x1, local copies, waits for them, and re-layouts: none -> 8.11 us  [rows_first(): jnp.stack([both] * lax.axis_size(axis))]
    all_gather x1 -> x0, waiting for transfers between devices: 5.85 us -> none  [rows_first(): out = lax.all_gather(both, axis, axis=0, tiled=True)]
    unnamed x21 -> x23, local copies, waits for them, and re-layouts: 15.3 us -> 14.8 us
  transfers between devices with their start and end apart: 1 -> 1, of which waited for: 1 -> 0; matrix products, arithmetic and copies ran while one was open for 0% -> 0% of each run, Pallas kernels for 0% -> 0%
where the time goes in v1:
time: 427 us
  blocking collectives  371 us (87%)
  local copies, waits for them, and re-layouts  42.5 us (10%)
  starting transfers between devices  9.25 us (2%)
    unnamed x1, blocking collectives  371 us
    transpose x1, local copies, waits for them, and re-layouts, rows_first(): jnp.moveaxis(b.reshape(-1, *t.shape[1:]), 0, dim)  16.2 us
    unnamed x23, local copies, waits for them, and re-layouts  14.8 us
    all_to_all x1, starting transfers between devices, rows_first(): lax.all_to_all(jnp.stack([both] * lax.axis_size(axis)), axis, 0, 0)  9.25 us
  transfers between devices with their start and end apart: 1, of which 0 were waited for; matrix products, arithmetic and copies ran while one was open for 0% of the time, Pallas kernels for 0%

profile of v1, /device:TPU:1, one launch (start us, length us, event | category | flops | bytes accessed | tf_op | source)
XLA Modules:
  0.0 426.7 jit_solution(4948037981632056475)
XLA Ops:
  0.6 0.0 copy-start
  0.7 0.0 copy-start.5
  0.7 0.0 copy-start.7
  0.7 0.0 copy-start.3
  0.7 0.0 copy-start.6
  0.7 0.0 copy-start.4
  0.7 0.0 copy-start.2
  0.7 0.8 copy-done
  1.5 1.5 fusion.4
  3.0 1.1 fusion.8
  4.1 0.0 copy-done.5
  4.1 0.0 copy-done.7
  4.1 0.0 copy-done.3
  4.1 0.2 fusion.7
  4.3 0.0 copy-done.6
  4.3 0.0 copy-done.4
  4.4 0.0 copy-done.2
  4.4 0.4 fusion.2
  4.7 0.1 pad_maximum_fusion
  4.8 8.1 %stack.2 = bf16[16,320,2304]{2,1,0:T(8,128)(2,1)} broadcast(bf16[320,2304]{1,0:T(8,128)(2,1)S(1)} %pad_maximum_fusion), dimensions={1,2} | broadcast | bytes 25067520 | tf_op jit(solution)/shard_map/stack | solution.py:14
  12.9 0.0 copy-start.8
  12.9 0.0 copy-start.9
  13.0 9.3 %all-to-all-start = ((bf16[16,320,2304]{2,1,0:T(8,128)(2,1)}), bf16[16,320,2304]{2,1,0:T(8,128)(2,1)}, u32[]{:S(2)}, u32[]{:S(2)}) async-start(bf16[16,320,2304]{2,1,0:T(8,128)(2,1)} %stack.2), calls=%async_computation | async-start | bytes 47185920 | tf_op jit(solution)/shard_map/all_to_all | solution.py:14
  22.2 0.0 copy-done.8
  22.2 0.0 copy-done.9
  22.2 0.2 dynamic-update-slice
  22.5 370.9 %all-reduce = bf16[5120]{0:T(1024)(128)(2,1)} all-reduce(bf16[5120]{0:T(1024)(128)(2,1)S(1)} %dynamic-update-slice), channel_id=1, replica_groups=mesh['shard'=16,'tp'=8] {'shard','tp'}, use_global_device_ids=true, to_apply=%add | all-reduce | flops 5120 | bytes 20480
  393.4 0.0 all-to-all-done
  393.4 16.2 %slice_bitcast_fusion = (bf16[1024,5120]{0,1:T(8,128)(2,1)}, bf16[5120,1024]{1,0:T(8,128)(2,1)}) fusion(bf16[5120,2304]{1,0:T(8,128)(2,1)} %bitcast.1), kind=kLoop, calls=%fused_computation | loop fusion | bytes 41943040 | tf_op jit(solution)/shard_map/transpose | solution.py:19
  409.6 3.4 fusion.9
  413.0 13.7 %copy.23 = bf16[1024,5120]{1,0:T(8,128)(2,1)} copy(bf16[1024,5120]{0,1:T(8,128)(2,1)} %get-tuple-element.15) | data formatting | bytes 20971520
  426.7 0.0 copy-done.1
  (3 shorter events, 0.0 us)
Async XLA Ops:
  0.6 0.8 copy-start
  0.7 3.4 copy-start.5
  0.7 3.4 copy-start.7
  0.7 3.4 copy-start.3
  0.7 3.7 copy-start.6
  0.7 3.7 copy-start.4
  0.7 3.7 copy-start.2
  12.9 9.3 %copy-start.8 = (f32[40]{0:T(128)S(1)}, f32[40]{0:T(128)}, u32[]{:S(2)}) copy-start(f32[40]{0:T(128)} %param.26) | copy-start | bytes 484
  12.9 9.3 %copy-start.9 = (f32[40]{0:T(128)S(1)}, f32[40]{0:T(128)}, u32[]{:S(2)}) copy-start(f32[40]{0:T(128)} %param.27) | copy-start | bytes 484
  13.0 380.4 %all-to-all-start = ((bf16[16,320,2304]{2,1,0:T(8,128)(2,1)}), bf16[16,320,2304]{2,1,0:T(8,128)(2,1)}, u32[]{:S(2)}, u32[]{:S(2)}) async-start(bf16[16,320,2304]{2,1,0:T(8,128)(2,1)} %stack.2), calls=%async_computation | async-start | bytes 47185920 | tf_op jit(solution)/shard_map/all_to_all | solution.py:14
  413.0 13.7 %copy-start.1 = (bf16[1024,32]{0,1:T(8,128)(2,1)S(1)}, bf16[1024,32]{0,1:T(8,128)(2,1)}, u32[]{:S(2)}) copy-start(bf16[1024,32]{0,1:T(8,128)(2,1)} %param.24) | copy-start | bytes 196612
